TPU v7x, 32 devices: a whole 2x2x4 slice. The times are simulated.
32 devices in a mesh: blk: 8 (over z, y), grp: 4 (over x, core).
Axes of the slice: x: 2, y: 2, z: 4, core: 2. Of those that a mesh axis runs over, the one named last changes fastest.
Arguments:
- embeddings: bfloat16 [4096, 1024], P(('blk', 'grp')), may hold values from -100 to 100
- labels: int32 [4096], P(('blk', 'grp')), may hold values from 0 to 4999, as said below
Outputs:
- anchor_loss: float32 [1024], P(('blk', 'grp'))
- mean_loss: float32 [], replicated
Inputs may be any that keep to these rules, and one draw needn't show every extreme that they name: `labels`: A label of 1000 or more belongs to one sample only.
All inputs are finite; a program needn't handle non-finite values.
Results may differ from a plain program's by a relative error of at most 0.0003.
Values may be sent and summed in bfloat16 or wider, within the bound.
A program may use at most 64 MiB of HBM per device.

v0:
```python
import jax
import jax.numpy as jnp
from jax import lax
from jax.sharding import PartitionSpec as P

A_DEV = 32


def make_fold(anchors, anchor_labels, anchor_ids, key_id_of):

    def fold(carry, pieces, start):
        keys, key_labels = pieces
        where_at = jnp.arange(keys.shape[0], dtype=jnp.int32)
        key_ids = key_id_of(where_at)
        score = (
            lax.dot_general(
                anchors, keys, (((1,), (1,)), ((), ())), preferred_element_type=jnp.float32
            )
            * 10.0
        )
        self_mask = anchor_ids[:, None] == key_ids[None, :]
        expo = jnp.where(self_mask, 0.0, jnp.exp(score - 10.0))
        positive = (anchor_labels[:, None] == key_labels[None, :]) & jnp.logical_not(self_mask)
        return (
            jnp.sum(expo, axis=1),
            jnp.sum(jnp.where(positive, score, 0.0), axis=1),
            jnp.sum(positive.astype(jnp.float32), axis=1),
        )

    return fold


def local(embeddings, labels):
    rows = embeddings.shape[0]
    values = embeddings.astype(jnp.float32)
    unit = (values * lax.rsqrt(jnp.sum(values * values, axis=1, keepdims=True) + 1e-06)).astype(
        jnp.bfloat16
    )
    own_anchors = unit[:A_DEV]
    own_labels = labels[:A_DEV]
    blk_index = lax.axis_index("blk")
    grp_index = lax.axis_index("grp")
    grp_count = lax.axis_size("grp")

    def strided_key(where_at):
        return (where_at // rows * grp_count + grp_index) * rows + where_at % rows

    positions = jnp.arange(A_DEV * grp_count, dtype=jnp.int32)
    anchors, anchor_labels = (
        lax.all_gather(own_anchors, "grp", axis=0, tiled=True),
        lax.all_gather(own_labels, "grp", axis=0, tiled=True),
    )
    anchor_ids = (blk_index * grp_count + positions // A_DEV) * rows + positions % A_DEV
    zeros = jnp.zeros((anchors.shape[0],), jnp.float32)
    fold = make_fold(anchors, anchor_labels, anchor_ids, strided_key)
    totals = fold(
        (zeros, zeros, zeros),
        (
            lax.all_gather(unit, "blk", axis=0, tiled=True),
            lax.all_gather(labels, "blk", axis=0, tiled=True),
        ),
        jnp.int32(0),
    )
    denom, pos_sum, count = (
        lax.psum_scatter(totals[0], "grp", scatter_dimension=0, tiled=True),
        lax.psum_scatter(totals[1], "grp", scatter_dimension=0, tiled=True),
        lax.psum_scatter(totals[2], "grp", scatter_dimension=0, tiled=True),
    )
    valid = count > 0.0
    anchor_loss = jnp.where(valid, jnp.log(denom) + 10.0 - pos_sum / jnp.maximum(count, 1.0), 0.0)
    loss_total, valid_total = lax.psum(
        (jnp.sum(anchor_loss), jnp.sum(valid.astype(jnp.float32))), ("blk", "grp")
    )
    mean_loss = loss_total / jnp.maximum(valid_total, 1.0)
    return (anchor_loss, mean_loss)


def solution(mesh):
    placed = (P(("blk", "grp"), None), P(("blk", "grp")))
    return jax.shard_map(
        local, mesh=mesh, in_specs=placed, out_specs=(P(("blk", "grp")), P()), check_vma=False
    )
```

profile of v0, /device:TPU:0, one launch (start us, length us, event | category | flops | bytes accessed | tf_op | source)
XLA Modules:
  0.0 120.6 jit_solution(12838552396629161836)
XLA Ops:
  7.2 0.0 all-gather.3.cloned.1.call-start
  7.2 1.1 fusion
  8.3 1.8 %fusion.1 = bf16[128,1024]{1,0:T(8,128)(2,1)} fusion(bf16[128,1024]{1,0:T(8,128)(2,1)} %param.2, f32[128]{0:T(128)S(1)} %add_rsqrt_fusion), kind=kLoop, calls=%fused_computation.6 | loop fusion | flops 393216 | bytes 524800 | tf_op jit(solution)/shard_map/convert_element_type | solution.py:36
  10.1 0.0 all-gather.3.cloned.1.call-update
  10.1 0.8 slice.8
  11.0 1.3 %fusion.22 = (u32[1]{0:T(128)}, u32[1]{0:T(128)}) fusion(u32[32]{0:T(128)} %constant.88, u32[]{:T(128)S(6)} %add.107, u32[]{:T(128)S(6)} %add.104), kind=kLoop, calls=%fused_computation.44 | loop fusion | bytes 24
  13.6 0.8 slice_dynamic-update-slice_fusion
  14.4 6.4 %all-reduce = s32[128]{0:T(128)S(1)} all-reduce(s32[128]{0:T(128)S(1)} %slice_dynamic-update-slice_fusion), channel_id=1, replica_groups=mesh['blk'=8,'grp'=4] {'grp'}, use_global_device_ids=true, to_apply=%add | all-reduce | flops 128 | bytes 1024
  20.7 21.0 %all-gather = s32[8,1,128]{2,1,0:T(1,128)S(1)} all-gather(s32[1,1,128]{2,1,0:T(1,128)} %bitcast.7), channel_id=1, replica_groups=mesh['blk'=8,'grp'=4] {'blk'}, dimensions={0}, use_global_device_ids=true | all-gather | bytes 4608 | tf_op jit(solution)/shard_map/all_gather | solution.py:60
  41.7 5.8 %all_gather.14 = bf16[128,1024]{1,0:T(8,128)(2,1)S(1)} all-gather(bf16[32,1024]{1,0:T(8,128)(2,1)S(1)} %slice.8), channel_id=1, replica_groups=mesh['blk'=8,'grp'=4] {'grp'}, dimensions={0}, use_global_device_ids=true | all-gather | bytes 327680 | tf_op jit(solution)/shard_map/all_gather | solution.py:50
  47.5 14.6 %all-gather.3.cloned.1.call-done = bf16[1024,1024]{1,0:T(8,128)(2,1)} async-done(((bf16[128,1024]{1,0:T(8,128)(2,1)}), bf16[1024,1024]{1,0:T(8,128)(2,1)}) %all-gather.3.cloned.1.call-update) | async-done | bytes 2097168 | tf_op jit(solution)/shard_map/all_gather | solution.py:59
  62.1 2.6 %fusion.2 = (f32[128]{0:T(128)S(1)}, f32[128]{0:T(128)S(1)}, f32[128]{0:T(128)S(1)}) fusion(s32[1024]{0:T(1024)S(1)} %fusion.13, s32[128]{0:T(128)S(1)} %fusion.15, s32[1024]{0:T(1024)S(1)} %bitcast.6, s32[128]{0:T(128)S(1)} %all-reduce, bf16[128,1024]{1,0:T(8,128)(2,1)S(1)} %all_gather.14, bf16[1024,1024]{1,0:T(8,128)(2,1)} %all-gather.3.cloned.1.call-done), kind=kOutput, calls=%fused_computation.7 | convolution fusion | flops 270007936 | bytes 2370048 | tf_op jit(solution)/shard_map/dot_general | solution.py:16
  64.8 5.7 %all-reduce.5 = (f32[128]{0:T(128)S(1)}, f32[128]{0:T(128)S(1)}, f32[128]{0:T(128)S(1)}) all-reduce(f32[128]{0:T(128)S(1)} %get-tuple-element.3, f32[128]{0:T(128)S(1)} %get-tuple-element.2, f32[128]{0:T(128)S(1)} %get-tuple-element.4), channel_id=4, replica_groups=mesh['blk'=8,'grp'=4] {'grp'}, use_global_device_ids=true, to_apply=%region_6.7.clone | all-reduce | flops 384 | bytes 3072
  70.4 1.3 %fusion.21 = (f32[]{:T(128)}, f32[32]{0:T(128)}, f32[]{:T(128)}) fusion(f32[128]{0:T(128)S(1)} %get-tuple-element.7, u32[]{:T(128)S(6)} %multiply.4, f32[128]{0:T(128)S(1)} %get-tuple-element.8, f32[128]{0:T(128)S(1)} %get-tuple-element.9), kind=kLoop, calls=%fused_computation.43 | loop fusion | flops 286 | bytes 524 | tf_op jit(solution)/shard_map/reduce_sum | solution.py:72
  71.7 39.7 %all-reduce.4 = (f32[]{:T(128)}, f32[]{:T(128)}) all-reduce(f32[]{:T(128)} %get-tuple-element.10, f32[]{:T(128)} %get-tuple-element.12), channel_id=1, replica_groups=mesh['blk'=8,'grp'=4] {'blk','grp'}, use_global_device_ids=true, to_apply=%region_8.9 | all-reduce | flops 2 | bytes 16 | tf_op jit(solution)/shard_map/psum | solution.py:71
  (4 shorter events, 0.0 us)
Async XLA Ops:
  7.2 54.9 %all-gather.3.cloned.1.call-start = ((), (), s32[]{:S(2)}) async-start(), calls=%async_computation | async-start | bytes 2359296 | tf_op jit(solution)/shard_map/all_gather | solution.py:59
Sparse Core Ops, SparseCore 0:
  10.2 51.8 all-gather.2
where the time goes:
time: 121 us
  blocking collectives  78.5 us (65%)
  between operations  17.7 us (15%)
  waiting for transfers between devices  14.6 us (12%)
  other arithmetic  4.18 us (3%)
  local copies, waits for them, and re-layouts  2.92 us (2%)
  matrix products  2.65 us (2%)
    psum x1, blocking collectives, local(): lax.psum((jnp.sum(anchor_loss), jnp.sum(valid.astype(jnp.float32))), ('bl...  39.7 us
    all_gather x1, blocking collectives, local(): lax.all_gather(labels, 'blk', axis=0, tiled=True)  21 us
    all_gather x1, waiting for transfers between devices, local(): lax.all_gather(unit, 'blk', axis=0, tiled=True)  14.6 us
    unnamed x2, blocking collectives  12 us
    all_gather x1, blocking collectives, local(): lax.all_gather(own_anchors, 'grp', axis=0, tiled=True)  5.76 us
    dot_general x1, matrix products, fold(): lax.dot_general(anchors, keys, (((1,), (1,)), ((), ())), preferred_elemen...  2.65 us
  transfers between devices with their start and end apart: 1, of which 1 were waited for; matrix products, arithmetic and copies ran while one was open for 2% of the time, Pallas kernels for 0%

commit v1 on v0

--- a/solution.py
+++ b/solution.py
@@ -4,6 +4,12 @@
 from jax.sharding import PartitionSpec as P
 
 A_DEV = 32
+
+
+def put_joints_up(target):
+    k_now = jax.lax.psum(target, "grp")
+    oldest = jax.lax.psum(k_now, "blk")
+    return oldest
 
 
 def make_fold(anchors, anchor_labels, anchor_ids, key_id_of):
@@ -68,8 +74,8 @@
     )
     valid = count > 0.0
     anchor_loss = jnp.where(valid, jnp.log(denom) + 10.0 - pos_sum / jnp.maximum(count, 1.0), 0.0)
-    loss_total, valid_total = lax.psum(
-        (jnp.sum(anchor_loss), jnp.sum(valid.astype(jnp.float32))), ("blk", "grp")
+    loss_total, valid_total = put_joints_up(
+        (jnp.sum(anchor_loss), jnp.sum(valid.astype(jnp.float32)))
     )
     mean_loss = loss_total / jnp.maximum(valid_total, 1.0)
     return (anchor_loss, mean_loss)

time: 121 us -> 108 us (0.89)
  blocking collectives: 78.5 us -> 65.7 us
    psum x1 -> x2, blocking collectives: 39.7 us -> 26.9 us  [the longest x1 19.6 us: put_joints_up(): oldest = jax.lax.psum(k_now, 'blk')]
  transfers between devices with their start and end apart: 1 -> 1, of which waited for: 1 -> 1; matrix products, arithmetic and copies ran while one was open for 2% -> 3% of each run, Pallas kernels for 0% -> 0%
where the time goes in v1:
time: 108 us
  blocking collectives  65.7 us (61%)
  between operations  17.7 us (16%)
  waiting for transfers between devices  14.6 us (14%)
  other arithmetic  4.09 us (4%)
  local copies, waits for them, and re-layouts  2.92 us (3%)
  matrix products  2.65 us (2%)
    all_gather x1, blocking collectives, local(): lax.all_gather(labels, 'blk', axis=0, tiled=True)  21 us
    psum x1, blocking collectives, put_joints_up(): oldest = jax.lax.psum(k_now, 'blk')  19.6 us
    all_gather x1, waiting for transfers between devices, local(): lax.all_gather(unit, 'blk', axis=0, tiled=True)  14.6 us
    unnamed x2, blocking collectives  12 us
    psum x1, blocking collectives, put_joints_up(): k_now = jax.lax.psum(target, 'grp')  7.28 us
    all_gather x1, blocking collectives, local(): lax.all_gather(own_anchors, 'grp', axis=0, tiled=True)  5.76 us
    dot_general x1, matrix products, fold(): lax.dot_general(anchors, keys, (((1,), (1,)), ((), ())), preferred_elemen...  2.65 us
  transfers between devices with their start and end apart: 1, of which 1 were waited for; matrix products, arithmetic and copies ran while one was open for 3% of the time, Pallas kernels for 0%

profile of v1, /device:TPU:0, one launch (start us, length us, event | category | flops | bytes accessed | tf_op | source)
XLA Modules:
  0.0 107.7 jit_solution(8831264422006213549)
XLA Ops:
  7.2 0.0 all-gather.3.cloned.1.call-start
  7.2 1.1 %fusion = f32[128]{0:T(128)S(1)} fusion(bf16[128,1024]{1,0:T(8,128)(2,1)} %param.2), kind=kLoop, calls=%fused_computation.5 | loop fusion | flops 393088 | bytes 262656 | tf_op jit(solution)/shard_map/reduce_sum | solution.py:42
  8.3 1.8 %fusion.1 = bf16[128,1024]{1,0:T(8,128)(2,1)} fusion(bf16[128,1024]{1,0:T(8,128)(2,1)} %param.2, f32[128]{0:T(128)S(1)} %add_rsqrt_fusion), kind=kLoop, calls=%fused_computation.6 | loop fusion | flops 393216 | bytes 524800 | tf_op jit(solution)/shard_map/convert_element_type | solution.py:42
  10.1 0.0 all-gather.3.cloned.1.call-update
  10.1 0.8 slice.8
  11.0 1.3 %fusion.22 = (u32[1]{0:T(128)}, u32[1]{0:T(128)}) fusion(u32[32]{0:T(128)} %constant.88, u32[]{:T(128)S(6)} %add.111, u32[]{:T(128)S(6)} %add.108), kind=kLoop, calls=%fused_computation.44 | loop fusion | bytes 24
  13.6 0.8 slice_dynamic-update-slice_fusion
  14.4 6.4 %all-reduce = s32[128]{0:T(128)S(1)} all-reduce(s32[128]{0:T(128)S(1)} %slice_dynamic-update-slice_fusion), channel_id=1, replica_groups=mesh['blk'=8,'grp'=4] {'grp'}, use_global_device_ids=true, to_apply=%add | all-reduce | flops 128 | bytes 1024
  20.7 21.0 %all-gather = s32[8,1,128]{2,1,0:T(1,128)S(1)} all-gather(s32[1,1,128]{2,1,0:T(1,128)} %bitcast.7), channel_id=1, replica_groups=mesh['blk'=8,'grp'=4] {'blk'}, dimensions={0}, use_global_device_ids=true | all-gather | bytes 4608 | tf_op jit(solution)/shard_map/all_gather | solution.py:66
  41.7 5.8 %all_gather.14 = bf16[128,1024]{1,0:T(8,128)(2,1)S(1)} all-gather(bf16[32,1024]{1,0:T(8,128)(2,1)S(1)} %slice.8), channel_id=1, replica_groups=mesh['blk'=8,'grp'=4] {'grp'}, dimensions={0}, use_global_device_ids=true | all-gather | bytes 327680 | tf_op jit(solution)/shard_map/all_gather | solution.py:56
  47.5 14.6 %all-gather.3.cloned.1.call-done = bf16[1024,1024]{1,0:T(8,128)(2,1)} async-done(((bf16[128,1024]{1,0:T(8,128)(2,1)}), bf16[1024,1024]{1,0:T(8,128)(2,1)}) %all-gather.3.cloned.1.call-update) | async-done | bytes 2097168 | tf_op jit(solution)/shard_map/all_gather | solution.py:65
  62.1 2.6 %fusion.2 = (f32[128]{0:T(128)S(1)}, f32[128]{0:T(128)S(1)}, f32[128]{0:T(128)S(1)}) fusion(s32[1024]{0:T(1024)S(1)} %fusion.13, s32[128]{0:T(128)S(1)} %fusion.15, s32[1024]{0:T(1024)S(1)} %bitcast.6, s32[128]{0:T(128)S(1)} %all-reduce, bf16[128,1024]{1,0:T(8,128)(2,1)S(1)} %all_gather.14, bf16[1024,1024]{1,0:T(8,128)(2,1)} %all-gather.3.cloned.1.call-done), kind=kOutput, calls=%fused_computation.7 | convolution fusion | flops 270007936 | bytes 2370048 | tf_op jit(solution)/shard_map/dot_general | solution.py:22
  64.8 5.7 %all-reduce.6 = (f32[128]{0:T(128)S(1)}, f32[128]{0:T(128)S(1)}, f32[128]{0:T(128)S(1)}) all-reduce(f32[128]{0:T(128)S(1)} %get-tuple-element.3, f32[128]{0:T(128)S(1)} %get-tuple-element.2, f32[128]{0:T(128)S(1)} %get-tuple-element.4), channel_id=4, replica_groups=mesh['blk'=8,'grp'=4] {'grp'}, use_global_device_ids=true, to_apply=%region_6.7.clone | all-reduce | flops 384 | bytes 3072
  70.4 1.2 %fusion.21 = (f32[]{:T(128)}, f32[32]{0:T(128)}, f32[]{:T(128)}) fusion(f32[128]{0:T(128)S(1)} %get-tuple-element.9, u32[]{:T(128)S(6)} %multiply.4, f32[128]{0:T(128)S(1)} %get-tuple-element.10, f32[128]{0:T(128)S(1)} %get-tuple-element.11), kind=kLoop, calls=%fused_computation.43 | loop fusion | flops 286 | bytes 524 | tf_op jit(solution)/shard_map/reduce_sum | solution.py:78
  71.6 7.3 %all-reduce.5 = (f32[]{:T(128)}, f32[]{:T(128)}) all-reduce(f32[]{:T(128)} %get-tuple-element.12, f32[]{:T(128)} %get-tuple-element.14), channel_id=1, replica_groups=mesh['blk'=8,'grp'=4] {'grp'}, use_global_device_ids=true, to_apply=%region_8.9 | all-reduce | flops 2 | bytes 16 | tf_op jit(solution)/shard_map/psum | solution.py:10
  78.9 19.6 %all-reduce.4 = (f32[]{:T(128)}, f32[]{:T(128)}) all-reduce(f32[]{:T(128)} %get-tuple-element.7, f32[]{:T(128)} %get-tuple-element.8), channel_id=1, replica_groups=mesh['blk'=8,'grp'=4] {'blk'}, use_global_device_ids=true, to_apply=%region_9.10 | all-reduce | flops 2 | bytes 16 | tf_op jit(solution)/shard_map/psum | solution.py:11
  (4 shorter events, 0.0 us)
Async XLA Ops:
  7.2 54.9 %all-gather.3.cloned.1.call-start = ((), (), s32[]{:S(2)}) async-start(), calls=%async_computation | async-start | bytes 2359296 | tf_op jit(solution)/shard_map/all_gather | solution.py:65
Sparse Core Ops, SparseCore 0:
  10.2 51.8 all-gather.2

commit v2 on v0

--- a/solution.py
+++ b/solution.py
@@ -4,6 +4,13 @@
 from jax.sharding import PartitionSpec as P
 
 A_DEV = 32
+
+
+def gather_over(x, axis, d):
+    size = lax.axis_size(axis)
+    parts = jnp.stack([x for _ in range(size)])
+    parts = lax.all_to_all(parts, axis, split_axis=0, concat_axis=0)
+    return jnp.concatenate(parts, axis=d)
 
 
 def make_fold(anchors, anchor_labels, anchor_ids, key_id_of):
@@ -55,10 +62,7 @@
     fold = make_fold(anchors, anchor_labels, anchor_ids, strided_key)
     totals = fold(
         (zeros, zeros, zeros),
-        (
-            lax.all_gather(unit, "blk", axis=0, tiled=True),
-            lax.all_gather(labels, "blk", axis=0, tiled=True),
-        ),
+        (gather_over(unit, "blk", 0), lax.all_gather(labels, "blk", axis=0, tiled=True)),
         jnp.int32(0),
     )
     denom, pos_sum, count = (

time: 121 us -> 126 us (1.041)
  blocking collectives: 78.5 us -> 107 us
  waiting for transfers between devices: 14.6 us -> 0.01 us
  between operations: 17.7 us -> 4.33 us
  starting transfers between devices: 0.04 us -> 7.44 us
  matrix products: 2.65 us -> 1.06 us
    all_gather x1, blocking collectives: 21 us -> 42.6 us  [local(): lax.all_gather(labels, 'blk', axis=0, tiled=True)]
    all_gather x1 -> x0, waiting for transfers between devices: 14.6 us -> none  [local(): lax.all_gather(unit, 'blk', axis=0, tiled=True)]
    all_to_all x0 -> x1, starting transfers between devices: none -> 7.44 us  [gather_over(): parts = lax.all_to_all(parts, axis, split_axis=0, concat_axis=0)]
    psum x1, blocking collectives: 39.7 us -> 46.3 us  [local(): lax.psum((jnp.sum(anchor_loss), jnp.sum(valid.astype(jnp.float32))), ('bl...]
    another operation x0 -> x1, local copies, waits for them, and re-layouts: none -> 1.62 us  [gather_over(): parts = jnp.stack([x for _ in range(size)])]
    dot_general x1, matrix products: 2.65 us -> 1.06 us  [fold(): lax.dot_general(anchors, keys, (((1,), (1,)), ((), ())), preferred_elemen...]
    unnamed x3 -> x7, local copies, waits for them, and re-layouts: 2.07 us -> 0.7 us
  transfers between devices with their start and end apart: 1 -> 1, of which waited for: 1 -> 0; matrix products, arithmetic and copies ran while one was open for 2% -> 1% of each run, Pallas kernels for 0% -> 0%
where the time goes in v2:
time: 126 us; the launch traced here: 125 us
  blocking collectives  107 us (85%)
  starting transfers between devices  7.44 us (6%)
  between operations  4.33 us (3%)
  other arithmetic  3.45 us (3%)
  local copies, waits for them, and re-layouts  2.32 us (2%)
    psum x1, blocking collectives, local(): lax.psum((jnp.sum(anchor_loss), jnp.sum(valid.astype(jnp.float32))), ('bl...  46.3 us
    all_gather x1, blocking collectives, local(): lax.all_gather(labels, 'blk', axis=0, tiled=True)  42.6 us
    unnamed x2, blocking collectives  12 us
    all_to_all x1, starting transfers between devices, gather_over(): parts = lax.all_to_all(parts, axis, split_axis=0, concat_axis=0)  7.44 us
    all_gather x1, blocking collectives, local(): lax.all_gather(own_anchors, 'grp', axis=0, tiled=True)  5.76 us
  transfers between devices with their start and end apart: 1, of which 0 were waited for; matrix products, arithmetic and copies ran while one was open for 1% of the time, Pallas kernels for 0%

profile of v2, /device:TPU:0, one launch (start us, length us, event | category | flops | bytes accessed | tf_op | source)
XLA Modules:
  0.0 125.3 jit_solution(2691134075254960675)
XLA Ops:
  0.6 1.1 fusion
  1.7 1.1 fusion.1
  2.8 1.6 %stack.2 = bf16[8,128,1024]{2,1,0:T(8,128)(2,1)} broadcast(bf16[128,1024]{1,0:T(8,128)(2,1)S(1)} %fusion.1), dimensions={1,2} | broadcast | bytes 2359296 | tf_op jit(solution)/shard_map/stack | solution.py:11
  4.4 0.0 copy-start
  4.4 0.0 copy-start.1
  4.4 7.4 %all-to-all-start = ((bf16[8,128,1024]{2,1,0:T(8,128)(2,1)}), bf16[8,128,1024]{2,1,0:T(8,128)(2,1)S(1)}, u32[]{:S(2)}, u32[]{:S(2)}) async-start(bf16[8,128,1024]{2,1,0:T(8,128)(2,1)} %stack.2), calls=%async_computation | async-start | bytes 4194304 | tf_op jit(solution)/shard_map/all_to_all | solution.py:12
  11.9 0.0 copy-done
  11.9 0.6 fusion.22
  13.8 0.0 copy-done.1
  13.8 0.1 slice_dynamic-update-slice_fusion
  13.9 4.9 %all-reduce = s32[128]{0:T(128)S(1)} all-reduce(s32[128]{0:T(128)S(1)} %slice_dynamic-update-slice_fusion), channel_id=1, replica_groups=mesh['blk'=8,'grp'=4] {'grp'}, use_global_device_ids=true, to_apply=%add | all-reduce | flops 128 | bytes 1024
  18.8 42.6 %all-gather = s32[8,1,128]{2,1,0:T(1,128)S(1)} all-gather(s32[1,1,128]{2,1,0:T(1,128)S(1)} %bitcast.9), channel_id=1, replica_groups=mesh['blk'=8,'grp'=4] {'blk'}, dimensions={0}, use_global_device_ids=true | all-gather | bytes 4608 | tf_op jit(solution)/shard_map/all_gather | solution.py:65
  61.5 5.8 %all_gather.11 = bf16[128,1024]{1,0:T(8,128)(2,1)S(1)} all-gather(bf16[32,1024]{1,0:T(8,128)(2,1)S(1)} %slice.8), channel_id=1, replica_groups=mesh['blk'=8,'grp'=4] {'grp'}, dimensions={0}, use_global_device_ids=true | all-gather | bytes 327680 | tf_op jit(solution)/shard_map/all_gather | solution.py:57
  67.2 0.0 all-to-all-done
  67.2 1.1 fusion.2
  68.3 7.1 %all-reduce.5 = (f32[128]{0:T(128)S(1)}, f32[128]{0:T(128)S(1)}, f32[128]{0:T(128)S(1)}) all-reduce(f32[128]{0:T(128)S(1)} %get-tuple-element.3, f32[128]{0:T(128)S(1)} %get-tuple-element.2, f32[128]{0:T(128)S(1)} %get-tuple-element.4), channel_id=4, replica_groups=mesh['blk'=8,'grp'=4] {'grp'}, use_global_device_ids=true, to_apply=%region_6.7.clone | all-reduce | flops 384 | bytes 3072
  75.4 1.3 %fusion.21 = (f32[]{:T(128)}, f32[32]{0:T(128)}, f32[]{:T(128)}) fusion(f32[128]{0:T(128)S(1)} %get-tuple-element.7, u32[]{:T(128)S(6)} %multiply.4, f32[128]{0:T(128)S(1)} %get-tuple-element.8, f32[128]{0:T(128)S(1)} %get-tuple-element.9), kind=kLoop, calls=%fused_computation.43 | loop fusion | flops 286 | bytes 524 | tf_op jit(solution)/shard_map/reduce_sum | solution.py:76
  76.7 46.3 %all-reduce.4 = (f32[]{:T(128)}, f32[]{:T(128)}) all-reduce(f32[]{:T(128)} %get-tuple-element.10, f32[]{:T(128)} %get-tuple-element.12), channel_id=1, replica_groups=mesh['blk'=8,'grp'=4] {'blk','grp'}, use_global_device_ids=true, to_apply=%region_8.9 | all-reduce | flops 2 | bytes 16 | tf_op jit(solution)/shard_map/psum | solution.py:75
  (5 shorter events, 0.0 us)
Async XLA Ops:
  4.4 7.5 %copy-start = (u32[32]{0:T(128)S(1)}, u32[32]{0:T(128)}, u32[]{:S(2)}) copy-start(u32[32]{0:T(128)} %constant.88) | copy-start | bytes 388
  4.4 9.4 %copy-start.1 = (s32[128]{0:T(128)S(1)}, s32[128]{0:T(128)}, u32[]{:S(2)}) copy-start(s32[128]{0:T(128)} %param.3) | copy-start | bytes 1540
  4.4 62.8 %all-to-all-start = ((bf16[8,128,1024]{2,1,0:T(8,128)(2,1)}), bf16[8,128,1024]{2,1,0:T(8,128)(2,1)S(1)}, u32[]{:S(2)}, u32[]{:S(2)}) async-start(bf16[8,128,1024]{2,1,0:T(8,128)(2,1)} %stack.2), calls=%async_computation | async-start | bytes 4194304 | tf_op jit(solution)/shard_map/all_to_all | solution.py:12
